TPU v7x, 32 devices: a whole 2x2x4 slice. The times are simulated.
32 devices in a mesh: row: 4 (over z), col: 8 (over y, x, core).
Axes of the slice: x: 2, y: 2, z: 4, core: 2. Of those that a mesh axis runs over, the one named last changes fastest.
Arguments:
- working: float32 [16, 4, 256, 8, 8, 256], P(None, 'row', None, None, 'col'), may hold values from -6 to 6
- factor_panel: float32 [2, 16, 4, 256, 256], P(None, None, 'row'), may hold values from -0.12 to 2, as said below
Outputs:
- gram_part: float32 [16, 4, 256, 8, 8, 256], P(None, 'row', None, None, 'col')
- finished_columns: float32 [8, 4, 256, 8, 4, 512], P(None, None, None, 'col', 'row')
Inputs may be any that keep to these rules, and one draw needn't show every extreme that they name: factor_panel holds a lower-triangular factor: entries above the factor's diagonal are zero and its diagonal entries lie between 1 and 2.
All inputs are finite; a program needn't handle non-finite values.
Results may differ from a plain program's by a relative error of at most 0.0001.
Values sent between devices are 32-bit elements; how exact they have to be, the bound alone decides.
No kernel may reach another device: no remote copies, remote signals or barrier semaphores. Data moves between devices by JAX's collectives and lax.ppermute only.
A program may use at most 256 MiB of HBM per device.

v0:
```python
import jax
import jax.numpy as jnp
from jax import lax
from jax.sharding import PartitionSpec as P

BLK = 256
K = 30
STEPS = 2


def from_root(value, axis, source):
    kept = jnp.where(lax.axis_index(axis) == source, value, 0).astype(value.dtype)
    return lax.psum(kept, axis)


def per_device(working, factor_panel):
    row_count = lax.axis_size("row")
    col_count = lax.axis_size("col")
    row_index = lax.axis_index("row")
    blocks_rows = working.shape[0]
    width = working.shape[2]
    blocks_cols = working.shape[3]
    matrix_rows = working.reshape(blocks_rows, width, blocks_cols * width)
    global_block = jnp.arange(blocks_rows) * row_count + row_index
    solved_list = []
    for step_index in range(STEPS):
        target = K + step_index
        slab = matrix_rows[target // row_count]
        solve_target = K + step_index
        owner = solve_target % row_count
        diagonal = jnp.tril(factor_panel[step_index, solve_target // row_count, 0])
        diagonal = jnp.where(row_index == owner, diagonal, jnp.eye(width, dtype=jnp.float32))
        solve_solved = lax.linalg.triangular_solve(diagonal, slab, left_side=True, lower=True)
        solved = from_root(solve_solved, "row", owner)
        column_part = factor_panel[step_index, :, 0]
        eliminate_target = K + step_index
        updated = matrix_rows - jnp.einsum(
            "rab,bc->rac", column_part, solved, precision=lax.Precision.HIGHEST
        )
        below = (global_block > eliminate_target)[:, None, None]
        here = (global_block == eliminate_target)[:, None, None]
        matrix_rows = jnp.where(below, updated, jnp.where(here, solved[None], matrix_rows))
        solved_list.append(solved)
    stacked = jnp.concatenate(solved_list, 0)
    depth = stacked.shape[0]
    owners_count = col_count // row_count
    pieces = [
        from_root(stacked.reshape(depth, blocks_cols, width), "col", row_index + offset * row_count)
        for offset in range(owners_count)
    ]
    chosen = jnp.stack(pieces, 2)
    row_panels = chosen.reshape(depth, blocks_rows * width)
    gram = lax.dot_general(
        row_panels, stacked, (((0,), (0,)), ((), ())), precision=lax.Precision.HIGHEST
    )
    gram = (gram * (1.0 / (STEPS * BLK))).reshape(blocks_rows, 1, width, blocks_cols, 1, width)
    finished_count = (K + STEPS) // row_count
    finished = matrix_rows[:finished_count].reshape(finished_count, 1, width, 1, row_count, -1)
    moved = lax.all_to_all(finished, "row", split_axis=4, concat_axis=1, tiled=True)
    return (gram, moved)


def solution(mesh):
    placed = (P(None, "row", None, None, "col", None), P(None, None, "row", None, None))
    return jax.shard_map(
        per_device,
        mesh=mesh,
        in_specs=placed,
        out_specs=(
            P(None, "row", None, None, "col", None),
            P(None, None, None, "col", "row", None),
        ),
        check_vma=False,
    )
```

profile of v0, /device:TPU:0, one launch (start us, length us, event | category | flops | bytes accessed | tf_op | source)
XLA Modules:
  0.0 810.8 jit_solution(15085424552516502196)
XLA Ops:
  7.2 1.1 fusion.9
  8.3 0.1 broadcast.96
  8.4 4.0 while.4
  8.4 0.6 fusion.24
  9.0 1.4 bitcast_dynamic-update-slice_fusion.4
  10.4 0.6 fusion.24
  11.0 1.4 bitcast_dynamic-update-slice_fusion.4
  12.4 19.7 %custom-call.4 = f32[2,128,128]{1,2,0:T(8,128)S(1)} custom-call(f32[2,128,128]{2,1,0:T(8,128)S(1)} %get-tuple-element.17), custom_call_target="InvertDiagBlocksLowerTriangular" | custom-call | tf_op jit(solution)/shard_map/triangular_solve/custom-call.1 | solution.py:33
  32.1 7.2 slice_reduce_fusion
  39.2 0.9 copy.44
  40.1 1.1 fusion.6
  41.2 1.0 convolution_subtract_fusion.1
  42.2 1.1 fusion.13
  43.3 1.5 maximum_select_fusion
  44.8 0.0 all-reduce.7.cloned.1.call-start
  44.8 79.1 %copy.24 = f32[16,1,256,8,1,256]{2,5,3,0,4,1:T(8,128)} copy(f32[16,1,256,8,1,256]{5,4,3,2,1,0:T(1,128)} %param.4) | data formatting | bytes 67108864 | tf_op args[0]
  123.9 3.8 while.5
  123.9 0.6 fusion.25
  124.5 1.3 bitcast_dynamic-update-slice_fusion.5
  125.8 0.6 fusion.25
  126.4 1.3 bitcast_dynamic-update-slice_fusion.5
  127.7 19.7 %custom-call.5 = f32[2,128,128]{1,2,0:T(8,128)S(1)} custom-call(f32[2,128,128]{2,1,0:T(8,128)S(1)} %get-tuple-element.18), custom_call_target="InvertDiagBlocksLowerTriangular" | custom-call | tf_op jit(solution)/shard_map/triangular_solve/custom-call.1 | solution.py:33
  147.4 1.9 copy.27
  149.3 73.5 %fusion = f32[16,256,2048]{1,2,0:T(8,128)} fusion(f32[16,256,2048]{1,2,0:T(8,128)} %bitcast.82, f32[256,2048]{0,1:T(8,128)S(1)} %copy.27, pred[16]{0:T(512)(128)(4,1)S(1)} %get-tuple-element.53, pred[16]{0:T(512)(128)(4,1)S(1)} %get-tuple-element.54, f32[2,16,1,256,256]{4,3,1,2,0:T(8,128)} %bitcast.86, f32[256,2048]{1,0:T(8,128)} %all-reduce.5.cloned.1.call-done), kind=kOutput, calls=%fused_computation.5 | convolution fusion | flops 25794969600 | bytes 75497504 | tf_op jit(solution)/shard_map/rab,bc->rac/dot_general | solution.py:37
  222.9 1.7 slice_bitcast_fusion.4
  224.6 1.1 fusion.4
  225.7 1.8 convolution_subtract_fusion
  227.5 1.1 fusion.11
  228.6 1.5 maximum_select_fusion.1
  230.1 89.0 %all-reduce.7.cloned.1.call-done = f32[256,2048]{1,0:T(8,128)} async-done(((f32[256,2048]{1,0:T(8,128)}), f32[256,2048]{1,0:T(8,128)}) %all-reduce.7.cloned.1.call-update) | async-done | bytes 2097168 | tf_op jit(solution)/shard_map/psum | solution.py:13
  319.1 58.3 %convolution_bitcast_fusion = f32[16,256,2048]{1,2,0:T(8,128)} fusion(f32[2,16,1,256,256]{4,3,1,2,0:T(8,128)} %bitcast.87, f32[256,2048]{1,0:T(8,128)} %all-reduce.7.cloned.1.call-done), kind=kOutput, calls=%fused_computation.6 | convolution fusion | flops 25769803776 | bytes 39845888 | tf_op jit(solution)/shard_map/rab,bc->rac/dot_general | solution.py:37
  377.4 1.8 copy.33
  379.2 18.5 %fusion.1 = f32[8,256,2048]{1,2,0:T(8,128)} fusion(f32[16,256,2048]{1,2,0:T(8,128)} %convolution_bitcast_fusion, f32[16,256,2048]{1,2,0:T(8,128)} %fusion, f32[256,2048]{0,1:T(8,128)} %copy.33, pred[8]{0:T(512)(128)(4,1)S(1)} %bitcast.93, pred[8]{0:T(512)(128)(4,1)S(1)} %bitcast.92), kind=kLoop, calls=%fused_computation.9 | loop fusion | flops 12582912 | bytes 52428816 | tf_op jit(solution)/shard_map/jit(_where)/select_n | solution.py:42
  397.8 16.4 %copy.34 = f32[8,1,256,1,4,512]{5,2,0,3,1,4:T(8,128)} copy(f32[8,1,256,1,4,512]{2,5,4,0,3,1:T(8,128)} %bitcast.83) | data formatting | bytes 33554432 | tf_op jit(solution)/shard_map/reshape | solution.py:58
  414.1 7.2 all-to-all-start
  421.3 0.0 all-reduce.9.cloned.1.call-start
  421.4 0.1 constant_dynamic-update-slice_fusion.1
  421.6 1.4 copy-done.2
  423.0 0.1 constant_dynamic-update-slice_fusion
  423.1 4.6 broadcast_select_fusion.1
  427.8 5.4 copy.41
  433.2 5.3 copy.42
  438.5 127.6 %all-reduce.9.cloned.1.call-done = (f32[512,8,1,256]{0,3,2,1:T(8,128)}, f32[512,8,1,256]{0,3,2,1:T(8,128)}) async-done(((f32[512,8,1,256]{0,3,2,1:T(8,128)}, f32[512,8,1,256]{0,3,2,1:T(8,128)}), (f32[512,8,1,256]{0,3,2,1:T(8,128)}, f32[512,8,1,256]{0,3,2,1:T(8,128)})) %all-reduce.9.cloned.1.call-update) | async-done | bytes 8388624 | tf_op jit(solution)/shard_map/psum | solution.py:13
  566.2 4.7 pad_maximum_fusion
  570.8 58.3 %convolution_multiply_fusion = f32[4096,2048]{1,0:T(8,128)} fusion(f32[512,4096]{0,1:T(8,128)S(1)} %bitcast.90, f32[512,2048]{1,0:T(8,128)S(1)} %copy-done.4), kind=kOutput, calls=%fused_computation.7 | convolution fusion | flops 51547996160 | bytes 46137344 | tf_op jit(solution)/shard_map/dot_general | solution.py:53
  629.2 48.3 %reshape.85 = f32[16,1,256,8,1,256]{5,4,3,2,1,0:T(1,128)} reshape(f32[4096,2048]{1,0:T(8,128)} %convolution_multiply_fusion) | data formatting | bytes 67108864 | tf_op jit(solution)/shard_map/reshape | solution.py:56
  677.5 106.6 %all-to-all-done = f32[8,1,256,1,4,512]{5,2,0,3,1,4:T(8,128)} async-done(((f32[8,1,256,1,4,512]{5,2,0,3,1,4:T(8,128)}), f32[8,1,256,1,4,512]{5,2,0,3,1,4:T(8,128)}, u32[]{:S(2)}, u32[]{:S(2)}) %all-to-all-start) | async-done | bytes 16777248 | tf_op jit(solution)/shard_map/all_to_all | solution.py:59
  784.1 19.9 %copy.36 = f32[8,4,256,1,1,512]{5,4,3,2,1,0:T(1,128)} copy(f32[8,4,256,1,1,512]{5,2,0,1,4,3:T(8,128)} %bitcast.22) | data formatting | bytes 33554432
  (23 shorter events, 0.2 us)
Async XLA Ops:
  7.2 140.2 %all-reduce.5.cloned.1.call-start = ((), (), s32[]{:S(2)}) async-start(), calls=%async_computation.1 | async-start | bytes 4194304 | tf_op jit(solution)/shard_map/psum | solution.py:13
  44.8 274.3 %all-reduce.7.cloned.1.call-start = ((), (), s32[]{:S(2)}) async-start(), calls=%async_computation.2 | async-start | bytes 4194304 | tf_op jit(solution)/shard_map/psum | solution.py:13
  319.1 58.3 %copy-start.1 = (f32[256,2048]{1,0:T(8,128)S(1)}, f32[256,2048]{1,0:T(8,128)}, u32[]{:S(2)}) copy-start(f32[256,2048]{1,0:T(8,128)} %all-reduce.7.cloned.1.call-done) | copy-start | bytes 6291460
  414.1 7.3 copy-start
  414.1 370.0 %all-to-all-start = ((f32[8,1,256,1,4,512]{5,2,0,3,1,4:T(8,128)}), f32[8,1,256,1,4,512]{5,2,0,3,1,4:T(8,128)}, u32[]{:S(2)}, u32[]{:S(2)}) async-start(f32[8,1,256,1,4,512]{5,2,0,3,1,4:T(8,128)} %copy.34), calls=%async_computation | async-start | bytes 33554432 | tf_op jit(solution)/shard_map/all_to_all | solution.py:59
  421.3 144.8 %all-reduce.9.cloned.1.call-start = ((), (), s32[]{:S(2)}) async-start(), calls=%async_computation.3 | async-start | bytes 16777216 | tf_op jit(solution)/shard_map/psum | solution.py:13
  421.4 1.6 copy-start.2
  423.1 4.7 copy-start.3
  566.2 4.7 copy-start.4
Sparse Core Ops, SparseCore 0:
  44.9 88.8 all-reduce.4
  230.2 88.8 all-reduce.6
  438.6 127.4 all-reduce.8
where the time goes:
time: 823 us; the launch traced here: 811 us
  waiting for transfers between devices  323 us (39%)
  local copies, waits for them, and re-layouts  197 us (24%)
  matrix products  197 us (24%)
  other arithmetic  71.2 us (9%)
  between operations  14.2 us (2%)
    psum x3, waiting for transfers between devices, from_root(): return lax.psum(kept, axis)  217 us
    dot_general x2, matrix products, per_device(): jnp.einsum('rab,bc->rac', column_part, solved, precision=lax.Precision.HI...  132 us
    all_to_all x1, waiting for transfers between devices, per_device(): lax.all_to_all(finished, 'row', split_axis=4, concat_axis=1, tiled=True)  107 us
    unnamed x14, local copies, waits for them, and re-layouts  101 us
    dot_general x1, matrix products, per_device(): lax.dot_general(row_panels, stacked, (((0,), (0,)), ((), ())), precision=...  58.3 us
    reshape x1, local copies, waits for them, and re-layouts, per_device(): (gram * (1.0 / (STEPS * BLK))).reshape(blocks_rows, 1, width, blocks_cols...  48.3 us
    another operation x4, other arithmetic, per_device(): lax.linalg.triangular_solve(diagonal, slab, left_side=True, lower=True)  40.4 us
    select_n x1, other arithmetic, per_device(): jnp.where(below, updated, jnp.where(here, solved[None], matrix_rows))  18.5 us
  transfers between devices with their start and end apart: 4, of which 3 were waited for; matrix products, arithmetic and copies ran while one was open for 28% of the time, Pallas kernels for 0%

commit v1 on v0

--- a/solution.py
+++ b/solution.py
@@ -56,7 +56,10 @@
     gram = (gram * (1.0 / (STEPS * BLK))).reshape(blocks_rows, 1, width, blocks_cols, 1, width)
     finished_count = (K + STEPS) // row_count
     finished = matrix_rows[:finished_count].reshape(finished_count, 1, width, 1, row_count, -1)
-    moved = lax.all_to_all(finished, "row", split_axis=4, concat_axis=1, tiled=True)
+    moved = jnp.concatenate(
+        lax.all_to_all(jnp.stack(jnp.split(finished, lax.axis_size("row"), axis=4)), "row", 0, 0),
+        axis=1,
+    )
     return (gram, moved)
 
 

time: 823 us -> 880 us (1.069)
  local copies, waits for them, and re-layouts: 197 us -> 239 us
  other arithmetic: 71.2 us -> 85.1 us
    unnamed x14 -> x19, local copies, waits for them, and re-layouts: 101 us -> 153 us
    another operation x0 -> x1, other arithmetic: none -> 20.4 us  [per_device(): jnp.stack(jnp.split(finished, lax.axis_size('row'), axis=4))]
    reshape x1 -> x0, local copies, waits for them, and re-layouts: 16.4 us -> none  [per_device(): matrix_rows[:finished_count]]
  transfers between devices with their start and end apart: 4 -> 4, of which waited for: 3 -> 3; matrix products, arithmetic and copies ran while one was open for 28% -> 26% of each run, Pallas kernels for 0% -> 0%
where the time goes in v1:
time: 880 us; the launch traced here: 866 us
  waiting for transfers between devices  323 us (37%)
  local copies, waits for them, and re-layouts  239 us (27%)
  matrix products  197 us (22%)
  other arithmetic  85.1 us (10%)
  between operations  14.3 us (2%)
    psum x3, waiting for transfers between devices, from_root(): return lax.psum(kept, axis)  217 us
    unnamed x19, local copies, waits for them, and re-layouts  153 us
    dot_general x2, matrix products, per_device(): jnp.einsum('rab,bc->rac', column_part, solved, precision=lax.Precision.HI...  132 us
    all_to_all x1, waiting for transfers between devices, per_device(): lax.all_to_all(jnp.stack(jnp.split(finished, lax.axis_size('row'), axis=4...  107 us
    dot_general x1, matrix products, per_device(): lax.dot_general(row_panels, stacked, (((0,), (0,)), ((), ())), precision=...  58.3 us
    reshape x1, local copies, waits for them, and re-layouts, per_device(): (gram * (1.0 / (STEPS * BLK))).reshape(blocks_rows, 1, width, blocks_cols...  48.3 us
    another operation x4, other arithmetic, per_device(): lax.linalg.triangular_solve(diagonal, slab, left_side=True, lower=True)  40.4 us
    another operation x1, other arithmetic, per_device(): jnp.stack(jnp.split(finished, lax.axis_size('row'), axis=4))  20.4 us
  transfers between devices with their start and end apart: 4, of which 3 were waited for; matrix products, arithmetic and copies ran while one was open for 26% of the time, Pallas kernels for 0%

profile of v1, /device:TPU:0, one launch (start us, length us, event | category | flops | bytes accessed | tf_op | source)
XLA Modules:
  0.0 866.5 jit_solution(17774296273174680836)
XLA Ops:
  7.2 1.1 fusion.9
  8.4 4.0 while.4
  8.4 0.6 fusion.25
  9.0 1.4 bitcast_dynamic-update-slice_fusion.4
  11.0 1.4 bitcast_dynamic-update-slice_fusion.4
  12.4 19.7 %custom-call.4 = f32[2,128,128]{1,2,0:T(8,128)S(1)} custom-call(f32[2,128,128]{2,1,0:T(8,128)S(1)} %get-tuple-element.17), custom_call_target="InvertDiagBlocksLowerTriangular" | custom-call | tf_op jit(solution)/shard_map/triangular_solve/custom-call.1 | solution.py:33
  32.1 7.2 slice_reduce_fusion
  39.2 0.9 copy.58
  40.1 1.1 fusion.6
  41.2 1.0 convolution_subtract_fusion.1
  42.2 1.1 fusion.13
  43.3 1.5 maximum_select_fusion
  44.8 79.1 %copy.30 = f32[16,1,256,8,1,256]{2,5,3,0,4,1:T(8,128)} copy(f32[16,1,256,8,1,256]{5,4,3,2,1,0:T(1,128)} %param.4) | data formatting | bytes 67108864 | tf_op args[0]
  124.0 3.8 while.5
  124.0 0.6 fusion.26
  124.6 1.3 bitcast_dynamic-update-slice_fusion.5
  125.9 0.6 fusion.26
  126.5 1.3 bitcast_dynamic-update-slice_fusion.5
  127.8 19.7 %custom-call.5 = f32[2,128,128]{1,2,0:T(8,128)S(1)} custom-call(f32[2,128,128]{2,1,0:T(8,128)S(1)} %get-tuple-element.18), custom_call_target="InvertDiagBlocksLowerTriangular" | custom-call | tf_op jit(solution)/shard_map/triangular_solve/custom-call.1 | solution.py:33
  147.5 1.9 copy.33
  149.5 73.5 %fusion = f32[16,256,2048]{1,2,0:T(8,128)} fusion(f32[16,256,2048]{1,2,0:T(8,128)} %bitcast.85, f32[256,2048]{0,1:T(8,128)S(1)} %copy.33, pred[16]{0:T(512)(128)(4,1)S(1)} %get-tuple-element.57, pred[16]{0:T(512)(128)(4,1)S(1)} %get-tuple-element.58, f32[2,16,1,256,256]{4,3,1,2,0:T(8,128)} %bitcast.94, f32[256,2048]{1,0:T(8,128)} %all-reduce.5.cloned.1.call-done), kind=kOutput, calls=%fused_computation.5 | convolution fusion | flops 25794969600 | bytes 75497504 | tf_op jit(solution)/shard_map/rab,bc->rac/dot_general | solution.py:37
  223.0 1.7 slice_bitcast_fusion.4
  224.7 1.1 fusion.4
  225.8 1.8 convolution_subtract_fusion
  227.6 1.1 fusion.11
  228.7 1.5 maximum_select_fusion.1
  230.2 89.0 %all-reduce.7.cloned.1.call-done = f32[256,2048]{1,0:T(8,128)} async-done(((f32[256,2048]{1,0:T(8,128)}), f32[256,2048]{1,0:T(8,128)}) %all-reduce.7.cloned.1.call-update) | async-done | bytes 2097168 | tf_op jit(solution)/shard_map/psum | solution.py:13
  319.2 58.3 %convolution_bitcast_fusion = f32[16,256,2048]{1,2,0:T(8,128)} fusion(f32[2,16,1,256,256]{4,3,1,2,0:T(8,128)} %bitcast.95, f32[256,2048]{1,0:T(8,128)} %all-reduce.7.cloned.1.call-done), kind=kOutput, calls=%fused_computation.6 | convolution fusion | flops 25769803776 | bytes 39845888 | tf_op jit(solution)/shard_map/rab,bc->rac/dot_general | solution.py:37
  377.5 1.8 copy.39
  379.3 12.1 %fusion.1 = f32[8,256,2048]{1,2,0:T(8,128)S(1)} fusion(f32[16,256,2048]{1,2,0:T(8,128)} %convolution_bitcast_fusion, f32[16,256,2048]{1,2,0:T(8,128)} %fusion, f32[256,2048]{0,1:T(8,128)} %copy.39, pred[8]{0:T(512)(128)(4,1)S(1)} %bitcast.101, pred[8]{0:T(512)(128)(4,1)S(1)} %bitcast.100), kind=kLoop, calls=%fused_computation.9 | loop fusion | flops 12582912 | bytes 52428816 | tf_op jit(solution)/shard_map/jit(_where)/select_n | solution.py:42
  391.4 6.0 fusion.16
  397.4 10.9 %copy.54 = f32[8,1,256,1,1,512]{5,4,3,2,1,0:T(1,128)} copy(f32[8,1,256,1,1,512]{2,5,4,0,3,1:T(8,128)} %get-tuple-element.47) | data formatting | bytes 8388608
  408.3 10.9 %copy.55 = f32[8,1,256,1,1,512]{5,4,3,2,1,0:T(1,128)} copy(f32[8,1,256,1,1,512]{2,5,4,0,3,1:T(8,128)} %get-tuple-element.49) | data formatting | bytes 8388608
  419.2 10.9 %copy.56 = f32[8,1,256,1,1,512]{5,4,3,2,1,0:T(1,128)} copy(f32[8,1,256,1,1,512]{2,5,4,0,3,1:T(8,128)} %get-tuple-element.48) | data formatting | bytes 8388608
  430.1 10.9 %copy.57 = f32[8,1,256,1,1,512]{5,4,3,2,1,0:T(1,128)} copy(f32[8,1,256,1,1,512]{2,5,4,0,3,1:T(8,128)} %get-tuple-element.50) | data formatting | bytes 8388608
  441.0 20.4 %pad_maximum_fusion = f32[4,8,1,256,1,1,512]{6,5,4,3,2,1,0:T(1,128)} fusion(f32[1,8,1,256,1,1,512]{6,5,4,3,2,1,0:T(1,128)} %bitcast.93, f32[1,8,1,256,1,1,512]{6,5,4,3,2,1,0:T(1,128)} %bitcast.92, f32[1,8,1,256,1,1,512]{6,5,4,3,2,1,0:T(1,128)} %bitcast.91, f32[1,8,1,256,1,1,512]{6,5,4,3,2,1,0:T(1,128)} %bitcast.90), kind=kLoop, calls=%fused_computation.10 | loop fusion | flops 12582912 | bytes 33554432 | tf_op jit(solution)/shard_map/stack | solution.py:60
  461.3 7.2 all-to-all-start
  468.8 1.4 copy-done.2
  470.4 4.6 broadcast_select_fusion.1
  475.0 5.4 copy.50
  480.4 5.3 copy.51
  485.7 127.7 %all-reduce.9.cloned.1.call-done = (f32[512,8,1,256]{0,3,2,1:T(8,128)}, f32[512,8,1,256]{0,3,2,1:T(8,128)}) async-done(((f32[512,8,1,256]{0,3,2,1:T(8,128)}, f32[512,8,1,256]{0,3,2,1:T(8,128)}), (f32[512,8,1,256]{0,3,2,1:T(8,128)}, f32[512,8,1,256]{0,3,2,1:T(8,128)})) %all-reduce.9.cloned.1.call-update) | async-done | bytes 8388624 | tf_op jit(solution)/shard_map/psum | solution.py:13
  613.4 4.7 pad_maximum_fusion.1
  618.1 58.3 %convolution_multiply_fusion = f32[4096,2048]{1,0:T(8,128)} fusion(f32[512,4096]{0,1:T(8,128)S(1)} %bitcast.98, f32[512,2048]{1,0:T(8,128)S(1)} %copy-done.4), kind=kOutput, calls=%fused_computation.7 | convolution fusion | flops 51547996160 | bytes 46137344 | tf_op jit(solution)/shard_map/dot_general | solution.py:53
  676.4 48.3 %reshape.93 = f32[16,1,256,8,1,256]{5,4,3,2,1,0:T(1,128)} reshape(f32[4096,2048]{1,0:T(8,128)} %convolution_multiply_fusion) | data formatting | bytes 67108864 | tf_op jit(solution)/shard_map/reshape | solution.py:56
  724.8 106.6 %all-to-all-done = f32[4,8,1,256,1,1,512]{6,5,4,3,2,1,0:T(1,128)} async-done(((f32[4,8,1,256,1,1,512]{6,5,4,3,2,1,0:T(1,128)}), f32[4,8,1,256,1,1,512]{6,5,4,3,2,1,0:T(1,128)}, u32[]{:S(2)}, u32[]{:S(2)}) %all-to-all-start) | async-done | bytes 16777248 | tf_op jit(solution)/shard_map/all_to_all | solution.py:60
  831.4 8.1 copy.60
  839.4 20.3 %copy.45 = f32[8,4,256,1,1,512]{5,4,3,2,1,0:T(1,128)} copy(f32[8,4,256,1,1,512]{5,2,0,1,4,3:T(8,128)S(1)} %bitcast.87) | data formatting | bytes 33554432
  (29 shorter events, 1.2 us)
Async XLA Ops:
  7.2 140.4 %all-reduce.5.cloned.1.call-start = ((), (), s32[]{:S(2)}) async-start(), calls=%async_computation.1 | async-start | bytes 4194304 | tf_op jit(solution)/shard_map/psum | solution.py:13
  44.8 274.4 %all-reduce.7.cloned.1.call-start = ((), (), s32[]{:S(2)}) async-start(), calls=%async_computation.2 | async-start | bytes 4194304 | tf_op jit(solution)/shard_map/psum | solution.py:13
  319.2 58.3 %copy-start.1 = (f32[256,2048]{1,0:T(8,128)S(1)}, f32[256,2048]{1,0:T(8,128)}, u32[]{:S(2)}) copy-start(f32[256,2048]{1,0:T(8,128)} %all-reduce.7.cloned.1.call-done) | copy-start | bytes 6291460
  461.3 7.3 copy-start
  461.3 370.0 %all-to-all-start = ((f32[4,8,1,256,1,1,512]{6,5,4,3,2,1,0:T(1,128)}), f32[4,8,1,256,1,1,512]{6,5,4,3,2,1,0:T(1,128)}, u32[]{:S(2)}, u32[]{:S(2)}) async-start(f32[4,8,1,256,1,1,512]{6,5,4,3,2,1,0:T(1,128)} %pad_maximum_fusion), calls=%async_computation | async-start | bytes 33554432 | tf_op jit(solution)/shard_map/all_to_all | solution.py:60
  468.6 144.8 %all-reduce.9.cloned.1.call-start = ((), (), s32[]{:S(2)}) async-start(), calls=%async_computation.3 | async-start | bytes 16777216 | tf_op jit(solution)/shard_map/psum | solution.py:13
  468.7 1.6 copy-start.2
  470.4 4.6 copy-start.3
  613.4 4.7 copy-start.4
Sparse Core Ops, SparseCore 0:
  44.9 88.8 all-reduce.4
  230.3 88.8 all-reduce.6
  485.9 127.4 all-reduce.8
